TPU v7x, 512 devices: a whole 4x8x8 slice. The times are simulated.
512 devices in a mesh: section: 32 (over x, y_hi, core), dp: 16 (over y_lo, z).
Axes of the slice: x: 4, y: 8 (y_hi: 4, y_lo: 2; y = y_hi * 2 + y_lo), z: 8, core: 2. Of those that a mesh axis runs over, the one named last changes fastest.
Arguments:
- out_pair: float32 [2048, 2048], P('dp'), may hold values from -6 to 6
- out_grad: bfloat16 [2048, 2048], P('dp'), may hold values from -6 to 6
- f_weight: bfloat16 [32, 1024, 1024], P('section', 'dp'), may hold values from -0.09375 to 0.09375
- g_weight: bfloat16 [32, 1024, 1024], P('section', 'dp'), may hold values from -0.09375 to 0.09375
- gains: float32 [32, 2, 1024], P('section'), may hold values from 0.1 to 1.9
Outputs:
- in_pair: float32 [32, 2048, 2048], P('section', 'dp')
- in_grad: bfloat16 [32, 2048, 2048], P('section', 'dp')
- f_grad: float32 [32, 1024, 1024], P('section', 'dp')
- g_grad: float32 [32, 1024, 1024], P('section', 'dp')
- gains_grad: float32 [32, 2, 1024], P('section')
All inputs are finite; a program needn't handle non-finite values.
Results may differ from a plain program's by a relative error of at most 0.04.
Values may be sent and summed in bfloat16 or wider, within the bound.
No kernel may reach another device: no remote copies, remote signals or barrier semaphores. Data moves between devices by JAX's collectives and lax.ppermute only.
A program may use at most 64 MiB of HBM per device.

v0:
```python
import jax
import jax.numpy as jnp
from jax import lax
from jax.sharding import PartitionSpec as P

offset = 0.25


def in_one_piece(arrays, axis, dim, along):
    widths = [a.shape[along] for a in arrays]
    both = jnp.concatenate(arrays, axis=along)
    result = lax.all_gather(both, axis, axis=dim, tiled=True)
    return tuple(jnp.split(result, [sum(widths[:k]) for k in range(1, len(widths))], axis=along))


def from_behind(array, axis, by):
    devices = lax.axis_size(axis)
    pairs = [(i, i + by) for i in range(devices) if 0 <= i + by < devices]
    return lax.ppermute(array, axis, pairs)


def sent_together(arrays, axis, dim, along):
    ends, at = ([], 0)
    for a in arrays[:-1]:
        at += a.shape[along]
        ends.append(at)
    both = jnp.concatenate(arrays, axis=along)
    return tuple(
        jnp.split(lax.psum_scatter(both, axis, scatter_dimension=dim, tiled=True), ends, axis=along)
    )


def silu_parts(pre_values):
    sigmoid_value = jax.nn.sigmoid(pre_values)
    return (pre_values * sigmoid_value, sigmoid_value * (1.0 + pre_values * (1.0 - sigmoid_value)))


def normalize(values, gain_row):
    inv_scale = lax.rsqrt(jnp.mean(values * values, axis=-1, keepdims=True) + offset)
    return ((values * inv_scale * gain_row).astype(jnp.bfloat16), inv_scale)


def norm_back(values, inv_scale, gain_row, upstream):
    weighted = gain_row * upstream
    cubed = inv_scale * inv_scale * inv_scale
    return inv_scale * weighted - values * cubed * jnp.mean(
        weighted * values, axis=-1, keepdims=True
    )


def times_transposed(delta, weight_full):
    return lax.dot_general(
        delta, weight_full, (((1,), (1,)), ((), ())), preferred_element_type=jnp.float32
    )


def coupling_back(upper_out, lower_out, upper_grad, lower_grad, w_first, w_second, gain_pair):
    normed_second, scale_second = normalize(upper_out, gain_pair[1])
    pre_second = jnp.dot(normed_second, w_second, preferred_element_type=jnp.float32)
    act_second, slope_second = silu_parts(pre_second)
    lower_in = lower_out - act_second
    normed_first, scale_first = normalize(lower_in, gain_pair[0])
    pre_first = jnp.dot(normed_first, w_first, preferred_element_type=jnp.float32)
    act_first, slope_first = silu_parts(pre_first)
    upper_in = upper_out - act_first
    delta_second = (lower_grad * slope_second).astype(jnp.bfloat16)
    back_second = times_transposed(delta_second, w_second)
    through = upper_grad + norm_back(upper_out, scale_second, gain_pair[1], back_second)
    delta_first = (through * slope_first).astype(jnp.bfloat16)
    back_first = times_transposed(delta_first, w_first)
    lower_total = lower_grad + norm_back(lower_in, scale_first, gain_pair[0], back_first)
    gain_terms = jnp.stack(
        [
            jnp.sum(back_first * lower_in * scale_first, axis=0),
            jnp.sum(back_second * upper_out * scale_second, axis=0),
        ]
    )
    return (
        upper_in,
        lower_in,
        through.astype(jnp.bfloat16),
        lower_total.astype(jnp.bfloat16),
        normed_first,
        delta_first,
        normed_second,
        delta_second,
        gain_terms,
    )


def shards(out_pair, out_grad, f_weight, g_weight, gains):
    sections = lax.axis_size("section")
    section_index = lax.axis_index("section")
    w_first, w_second = in_one_piece((f_weight[0], g_weight[0]), "dp", 0, 1)
    gain_pair = gains[0]
    row_count = out_pair.shape[0]
    pair_width = out_pair.shape[1]
    channels = pair_width // 2
    blocks = 8
    block_rows = row_count // blocks
    tick_count = blocks + sections - 1
    is_last = section_index == sections - 1

    def tick(tick_index, loop_state):
        pair_in, grad_in = (loop_state[0], loop_state[1])
        buffers = loop_state[2:]
        block_index = tick_index - (sections - 1 - section_index)
        active = jnp.logical_and(block_index >= 0, block_index < blocks)
        row_start = jnp.clip(block_index, 0, blocks - 1) * block_rows
        pair_here = jnp.where(
            is_last, lax.dynamic_slice_in_dim(out_pair, row_start, block_rows, 0), pair_in
        )
        grad_here = jnp.where(
            is_last, lax.dynamic_slice_in_dim(out_grad, row_start, block_rows, 0), grad_in
        )

        def compute(held):
            pair_buf, grad_buf, first_norms, first_deltas, second_norms, second_deltas, gain_acc = (
                held
            )
            results = coupling_back(
                pair_here[:, :channels],
                pair_here[:, channels:],
                grad_here[:, :channels].astype(jnp.float32),
                grad_here[:, channels:].astype(jnp.float32),
                w_first,
                w_second,
                gain_pair,
            )
            new_pair = jnp.concatenate([results[0], results[1]], axis=1)
            new_grad = jnp.concatenate([results[2], results[3]], axis=1)
            return (
                lax.dynamic_update_slice_in_dim(pair_buf, new_pair, row_start, 0),
                lax.dynamic_update_slice_in_dim(grad_buf, new_grad, row_start, 0),
                lax.dynamic_update_slice_in_dim(first_norms, results[4], row_start, 0),
                lax.dynamic_update_slice_in_dim(first_deltas, results[5], row_start, 0),
                lax.dynamic_update_slice_in_dim(second_norms, results[6], row_start, 0),
                lax.dynamic_update_slice_in_dim(second_deltas, results[7], row_start, 0),
                gain_acc + results[8],
                new_pair,
                new_grad,
            )

        def unchanged(held):
            return held + (
                jnp.zeros((block_rows, pair_width), jnp.float32),
                jnp.zeros((block_rows, pair_width), jnp.bfloat16),
            )

        updated = lax.cond(active, compute, unchanged, buffers)
        joined = jnp.concatenate([updated[7], updated[8].astype(jnp.float32)], axis=1)
        arrived = from_behind(joined.astype(jnp.bfloat16), "section", -1).astype(joined.dtype)
        sent_pair = arrived[:, :pair_width]
        sent_grad = arrived[:, pair_width:].astype(jnp.bfloat16)
        return (sent_pair, sent_grad) + updated[:7]

    initial = (
        jnp.zeros((block_rows, pair_width), jnp.float32),
        jnp.zeros((block_rows, pair_width), jnp.bfloat16),
        jnp.zeros((row_count, pair_width), jnp.float32),
        jnp.zeros((row_count, pair_width), jnp.bfloat16),
        jnp.zeros((row_count, channels), jnp.bfloat16),
        jnp.zeros((row_count, channels), jnp.bfloat16),
        jnp.zeros((row_count, channels), jnp.bfloat16),
        jnp.zeros((row_count, channels), jnp.bfloat16),
        jnp.zeros((2, channels), jnp.float32),
    )
    final_state = lax.fori_loop(0, tick_count, tick, initial)
    pair_buf, grad_buf, first_norms, first_deltas, second_norms, second_deltas, gain_acc = (
        final_state[2:]
    )
    contract_rows = (((0,), (0,)), ((), ()))
    first_part = lax.dot_general(
        first_norms, first_deltas, contract_rows, preferred_element_type=jnp.float32
    )
    second_part = lax.dot_general(
        second_norms, second_deltas, contract_rows, preferred_element_type=jnp.float32
    )
    first_sum, second_sum = tuple(
        (
            part.astype(jnp.float32)
            for part in sent_together(
                (first_part.astype(jnp.bfloat16), second_part.astype(jnp.bfloat16)), "dp", 0, 1
            )
        )
    )
    gain_total = lax.psum(gain_acc, "dp")
    return (pair_buf[None], grad_buf[None], first_sum[None], second_sum[None], gain_total[None])


def solution(mesh):
    placed = (
        P("dp", None),
        P("dp", None),
        P("section", "dp", None),
        P("section", "dp", None),
        P("section", None, None),
    )
    return jax.shard_map(
        shards,
        mesh=mesh,
        in_specs=placed,
        out_specs=(
            P("section", "dp", None),
            P("section", "dp", None),
            P("section", "dp", None),
            P("section", "dp", None),
            P("section", None, None),
        ),
        check_vma=False,
    )
```

profile of v0, /device:TPU:2, one launch (start us, length us, event | category | flops | bytes accessed | tf_op | source)
XLA Modules:
  0.0 722.4 jit_solution(5279875102858007164)
XLA Ops:
  9.0 85.5 %all-gather.2.cloned.1.call-done = bf16[1024,2048]{1,0:T(8,128)(2,1)} async-done(((bf16[64,2048]{1,0:T(8,128)(2,1)}), bf16[1024,2048]{1,0:T(8,128)(2,1)}) %all-gather.2.cloned.1.call-update) | async-done | bytes 4194320 | tf_op jit(solution)/shard_map/all_gather | solution.py:12
  100.6 506.6 %while.32 = (s32[]{:T(128)}, f32[16,2048]{1,0:T(8,128)S(1)}, bf16[16,2048]{1,0:T(8,128)(2,1)S(1)}, f32[128,2048]{1,0:T(8,128)}, bf16[128,2048]{1,0:T(8,128)(2,1)...) while((s32[]{:T(128)}, f32[16,2048]{1,0:T(8,128)S(1)}, ...), condition=%wide.region_9.10_spmd.clone, body=%wide.region_0.9_spmd.clone.sunk | while | flops 136267888 | bytes 20988308 | solution.py:168
  106.5 6.9 collective-permute-start
  116.1 6.9 collective-permute-start
  127.0 6.8 collective-permute-start
  136.5 6.9 collective-permute-start
  146.1 6.9 collective-permute-start
  155.6 6.8 collective-permute-start
  165.1 6.8 collective-permute-start
  193.4 6.8 collective-permute-start
  313.3 71.5 %collective-permute-done = bf16[16,4096]{1,0:T(8,128)(2,1)S(1)} collective-permute-done((bf16[16,4096]{1,0:T(8,128)(2,1)S(1)}, bf16[16,4096]{1,0:T(8,128)(2,1)S(1)}, u32[]{:S(2)}, u32[]{:S(2)}) %collective-permute-start) | collective-permute-done | bytes 131104 | tf_op jit(solution)/shard_map/while/body/eval_jaxpr/ppermute | solution.py:19
  384.9 7.9 %conditional.3 = (f32[128,2048]{1,0:T(8,128)}, bf16[128,2048]{1,0:T(8,128)(2,1)}, bf16[128,1024]{1,0:T(8,128)(2,1)S(1)}, bf16[128,1024]{1,0:T(8,128)(2,1)S(1)}, ...) conditional(s32[]{:T(128)} %convert_element_type.155, ...), branch_computations={%region_1.1_spmd, %region_2.8_spmd.clone} | conditional | flops 135972976 | bytes 19873738 | solution.py:150
  394.7 7.4 %collective-permute-done = bf16[16,4096]{1,0:T(8,128)(2,1)S(1)} collective-permute-done((bf16[16,4096]{1,0:T(8,128)(2,1)S(1)}, bf16[16,4096]{1,0:T(8,128)(2,1)S(1)}, u32[]{:S(2)}, u32[]{:S(2)}) %collective-permute-start) | collective-permute-done | bytes 131104 | tf_op jit(solution)/shard_map/while/body/eval_jaxpr/ppermute | solution.py:19
  402.1 7.9 %conditional.3 = (f32[128,2048]{1,0:T(8,128)}, bf16[128,2048]{1,0:T(8,128)(2,1)}, bf16[128,1024]{1,0:T(8,128)(2,1)S(1)}, bf16[128,1024]{1,0:T(8,128)(2,1)S(1)}, ...) conditional(s32[]{:T(128)} %convert_element_type.155, ...), branch_computations={%region_1.1_spmd, %region_2.8_spmd.clone} | conditional | flops 135972976 | bytes 19873738 | solution.py:150
  411.9 7.4 %collective-permute-done = bf16[16,4096]{1,0:T(8,128)(2,1)S(1)} collective-permute-done((bf16[16,4096]{1,0:T(8,128)(2,1)S(1)}, bf16[16,4096]{1,0:T(8,128)(2,1)S(1)}, u32[]{:S(2)}, u32[]{:S(2)}) %collective-permute-start) | collective-permute-done | bytes 131104 | tf_op jit(solution)/shard_map/while/body/eval_jaxpr/ppermute | solution.py:19
  419.3 7.9 %conditional.3 = (f32[128,2048]{1,0:T(8,128)}, bf16[128,2048]{1,0:T(8,128)(2,1)}, bf16[128,1024]{1,0:T(8,128)(2,1)S(1)}, bf16[128,1024]{1,0:T(8,128)(2,1)S(1)}, ...) conditional(s32[]{:T(128)} %convert_element_type.155, ...), branch_computations={%region_1.1_spmd, %region_2.8_spmd.clone} | conditional | flops 135972976 | bytes 19873738 | solution.py:150
  429.2 7.5 %collective-permute-done = bf16[16,4096]{1,0:T(8,128)(2,1)S(1)} collective-permute-done((bf16[16,4096]{1,0:T(8,128)(2,1)S(1)}, bf16[16,4096]{1,0:T(8,128)(2,1)S(1)}, u32[]{:S(2)}, u32[]{:S(2)}) %collective-permute-start) | collective-permute-done | bytes 131104 | tf_op jit(solution)/shard_map/while/body/eval_jaxpr/ppermute | solution.py:19
  436.7 7.9 %conditional.3 = (f32[128,2048]{1,0:T(8,128)}, bf16[128,2048]{1,0:T(8,128)(2,1)}, bf16[128,1024]{1,0:T(8,128)(2,1)S(1)}, bf16[128,1024]{1,0:T(8,128)(2,1)S(1)}, ...) conditional(s32[]{:T(128)} %convert_element_type.155, ...), branch_computations={%region_1.1_spmd, %region_2.8_spmd.clone} | conditional | flops 135972976 | bytes 19873738 | solution.py:150
  446.5 7.4 %collective-permute-done = bf16[16,4096]{1,0:T(8,128)(2,1)S(1)} collective-permute-done((bf16[16,4096]{1,0:T(8,128)(2,1)S(1)}, bf16[16,4096]{1,0:T(8,128)(2,1)S(1)}, u32[]{:S(2)}, u32[]{:S(2)}) %collective-permute-start) | collective-permute-done | bytes 131104 | tf_op jit(solution)/shard_map/while/body/eval_jaxpr/ppermute | solution.py:19
  453.9 7.9 %conditional.3 = (f32[128,2048]{1,0:T(8,128)}, bf16[128,2048]{1,0:T(8,128)(2,1)}, bf16[128,1024]{1,0:T(8,128)(2,1)S(1)}, bf16[128,1024]{1,0:T(8,128)(2,1)S(1)}, ...) conditional(s32[]{:T(128)} %convert_element_type.155, ...), branch_computations={%region_1.1_spmd, %region_2.8_spmd.clone} | conditional | flops 135972976 | bytes 19873738 | solution.py:150
  463.7 7.4 %collective-permute-done = bf16[16,4096]{1,0:T(8,128)(2,1)S(1)} collective-permute-done((bf16[16,4096]{1,0:T(8,128)(2,1)S(1)}, bf16[16,4096]{1,0:T(8,128)(2,1)S(1)}, u32[]{:S(2)}, u32[]{:S(2)}) %collective-permute-start) | collective-permute-done | bytes 131104 | tf_op jit(solution)/shard_map/while/body/eval_jaxpr/ppermute | solution.py:19
  471.1 7.9 %conditional.3 = (f32[128,2048]{1,0:T(8,128)}, bf16[128,2048]{1,0:T(8,128)(2,1)}, bf16[128,1024]{1,0:T(8,128)(2,1)S(1)}, bf16[128,1024]{1,0:T(8,128)(2,1)S(1)}, ...) conditional(s32[]{:T(128)} %convert_element_type.155, ...), branch_computations={%region_1.1_spmd, %region_2.8_spmd.clone} | conditional | flops 135972976 | bytes 19873738 | solution.py:150
  481.0 7.4 %collective-permute-done = bf16[16,4096]{1,0:T(8,128)(2,1)S(1)} collective-permute-done((bf16[16,4096]{1,0:T(8,128)(2,1)S(1)}, bf16[16,4096]{1,0:T(8,128)(2,1)S(1)}, u32[]{:S(2)}, u32[]{:S(2)}) %collective-permute-start) | collective-permute-done | bytes 131104 | tf_op jit(solution)/shard_map/while/body/eval_jaxpr/ppermute | solution.py:19
  488.4 7.9 %conditional.3 = (f32[128,2048]{1,0:T(8,128)}, bf16[128,2048]{1,0:T(8,128)(2,1)}, bf16[128,1024]{1,0:T(8,128)(2,1)S(1)}, bf16[128,1024]{1,0:T(8,128)(2,1)S(1)}, ...) conditional(s32[]{:T(128)} %convert_element_type.155, ...), branch_computations={%region_1.1_spmd, %region_2.8_spmd.clone} | conditional | flops 135972976 | bytes 19873738 | solution.py:150
  498.2 11.7 %collective-permute-done = bf16[16,4096]{1,0:T(8,128)(2,1)S(1)} collective-permute-done((bf16[16,4096]{1,0:T(8,128)(2,1)S(1)}, bf16[16,4096]{1,0:T(8,128)(2,1)S(1)}, u32[]{:S(2)}, u32[]{:S(2)}) %collective-permute-start) | collective-permute-done | bytes 131104 | tf_op jit(solution)/shard_map/while/body/eval_jaxpr/ppermute | solution.py:19
  510.0 7.9 %conditional.3 = (f32[128,2048]{1,0:T(8,128)}, bf16[128,2048]{1,0:T(8,128)(2,1)}, bf16[128,1024]{1,0:T(8,128)(2,1)S(1)}, bf16[128,1024]{1,0:T(8,128)(2,1)S(1)}, ...) conditional(s32[]{:T(128)} %convert_element_type.155, ...), branch_computations={%region_1.1_spmd, %region_2.8_spmd.clone} | conditional | flops 135972976 | bytes 19873738 | solution.py:150
  523.7 14.6 %collective-permute-start = (bf16[16,4096]{1,0:T(8,128)(2,1)S(1)}, bf16[16,4096]{1,0:T(8,128)(2,1)S(1)}, u32[]{:S(2)}, u32[]{:S(2)}) collective-permute-start(bf16[16,4096]{1,0:T(8,128)(2,1)S(1)} %pad_maximum_fusion.7), channel_id=1, source_target_pairs={{16,0},{32,16},{48,32},{64,48},{80,64},{96,80},{112,96},{128,112},... | collective-permute-start | bytes 393224 | tf_op jit(solution)/shard_map/while/body/eval_jaxpr/ppermute | solution.py:19
  541.1 6.8 collective-permute-start
  550.6 6.8 collective-permute-start
  597.7 6.9 collective-permute-start
  617.6 33.1 %psum.7 = f32[1,2,1024]{2,1,0:T(2,128)} all-reduce(f32[1,2,1024]{2,1,0:T(2,128)S(1)} %bitcast.40), channel_id=1, replica_groups=mesh['section'=32,'dp'=16] {'dp'}, use_global_device_ids=true, to_apply=%region_11.12 | all-reduce | flops 2048 | bytes 16384 | tf_op jit(solution)/shard_map/psum | solution.py:187
  650.7 61.6 %reduce-scatter.4.cloned.1.call-done = bf16[64,2048]{1,0:T(8,128)(2,1)} async-done(((bf16[1024,2048]{1,0:T(8,128)(2,1)}), bf16[64,2048]{1,0:T(8,128)(2,1)}) %reduce-scatter.4.cloned.1.call-update) | async-done | bytes 262160
  (417 shorter events, 308.2 us)
Async XLA Ops:
  7.2 87.4 %all-gather.2.cloned.1.call-start = ((), (), s32[]{:S(2)}) async-start(), calls=%async_computation.1 | async-start | bytes 4456448 | tf_op jit(solution)/shard_map/all_gather | solution.py:12
  8.9 703.4 %reduce-scatter.4.cloned.1.call-start = ((), (), s32[]{:S(2)}) async-start(), calls=%async_computation.2 | async-start | bytes 4456448
  106.5 9.4 %collective-permute-start = (bf16[16,4096]{1,0:T(8,128)(2,1)S(1)}, bf16[16,4096]{1,0:T(8,128)(2,1)S(1)}, u32[]{:S(2)}, u32[]{:S(2)}) collective-permute-start(bf16[16,4096]{1,0:T(8,128)(2,1)S(1)} %pad_maximum_fusion.7), channel_id=1, source_target_pairs={{16,0},{32,16},{48,32},{64,48},{80,64},{96,80},{112,96},{128,112},... | collective-permute-start | bytes 393224 | tf_op jit(solution)/shard_map/while/body/eval_jaxpr/ppermute | solution.py:19
  116.1 10.8 %collective-permute-start = (bf16[16,4096]{1,0:T(8,128)(2,1)S(1)}, bf16[16,4096]{1,0:T(8,128)(2,1)S(1)}, u32[]{:S(2)}, u32[]{:S(2)}) collective-permute-start(bf16[16,4096]{1,0:T(8,128)(2,1)S(1)} %pad_maximum_fusion.7), channel_id=1, source_target_pairs={{16,0},{32,16},{48,32},{64,48},{80,64},{96,80},{112,96},{128,112},... | collective-permute-start | bytes 393224 | tf_op jit(solution)/shard_map/while/body/eval_jaxpr/ppermute | solution.py:19
  127.0 9.4 %collective-permute-start = (bf16[16,4096]{1,0:T(8,128)(2,1)S(1)}, bf16[16,4096]{1,0:T(8,128)(2,1)S(1)}, u32[]{:S(2)}, u32[]{:S(2)}) collective-permute-start(bf16[16,4096]{1,0:T(8,128)(2,1)S(1)} %pad_maximum_fusion.7), channel_id=1, source_target_pairs={{16,0},{32,16},{48,32},{64,48},{80,64},{96,80},{112,96},{128,112},... | collective-permute-start | bytes 393224 | tf_op jit(solution)/shard_map/while/body/eval_jaxpr/ppermute | solution.py:19
  136.5 9.4 %collective-permute-start = (bf16[16,4096]{1,0:T(8,128)(2,1)S(1)}, bf16[16,4096]{1,0:T(8,128)(2,1)S(1)}, u32[]{:S(2)}, u32[]{:S(2)}) collective-permute-start(bf16[16,4096]{1,0:T(8,128)(2,1)S(1)} %pad_maximum_fusion.7), channel_id=1, source_target_pairs={{16,0},{32,16},{48,32},{64,48},{80,64},{96,80},{112,96},{128,112},... | collective-permute-start | bytes 393224 | tf_op jit(solution)/shard_map/while/body/eval_jaxpr/ppermute | solution.py:19
  146.1 9.4 %collective-permute-start = (bf16[16,4096]{1,0:T(8,128)(2,1)S(1)}, bf16[16,4096]{1,0:T(8,128)(2,1)S(1)}, u32[]{:S(2)}, u32[]{:S(2)}) collective-permute-start(bf16[16,4096]{1,0:T(8,128)(2,1)S(1)} %pad_maximum_fusion.7), channel_id=1, source_target_pairs={{16,0},{32,16},{48,32},{64,48},{80,64},{96,80},{112,96},{128,112},... | collective-permute-start | bytes 393224 | tf_op jit(solution)/shard_map/while/body/eval_jaxpr/ppermute | solution.py:19
  155.6 9.3 %collective-permute-start = (bf16[16,4096]{1,0:T(8,128)(2,1)S(1)}, bf16[16,4096]{1,0:T(8,128)(2,1)S(1)}, u32[]{:S(2)}, u32[]{:S(2)}) collective-permute-start(bf16[16,4096]{1,0:T(8,128)(2,1)S(1)} %pad_maximum_fusion.7), channel_id=1, source_target_pairs={{16,0},{32,16},{48,32},{64,48},{80,64},{96,80},{112,96},{128,112},... | collective-permute-start | bytes 393224 | tf_op jit(solution)/shard_map/while/body/eval_jaxpr/ppermute | solution.py:19
  165.1 9.3 %collective-permute-start = (bf16[16,4096]{1,0:T(8,128)(2,1)S(1)}, bf16[16,4096]{1,0:T(8,128)(2,1)S(1)}, u32[]{:S(2)}, u32[]{:S(2)}) collective-permute-start(bf16[16,4096]{1,0:T(8,128)(2,1)S(1)} %pad_maximum_fusion.7), channel_id=1, source_target_pairs={{16,0},{32,16},{48,32},{64,48},{80,64},{96,80},{112,96},{128,112},... | collective-permute-start | bytes 393224 | tf_op jit(solution)/shard_map/while/body/eval_jaxpr/ppermute | solution.py:19
  174.5 9.3 %collective-permute-start = (bf16[16,4096]{1,0:T(8,128)(2,1)S(1)}, bf16[16,4096]{1,0:T(8,128)(2,1)S(1)}, u32[]{:S(2)}, u32[]{:S(2)}) collective-permute-start(bf16[16,4096]{1,0:T(8,128)(2,1)S(1)} %pad_maximum_fusion.7), channel_id=1, source_target_pairs={{16,0},{32,16},{48,32},{64,48},{80,64},{96,80},{112,96},{128,112},... | collective-permute-start | bytes 393224 | tf_op jit(solution)/shard_map/while/body/eval_jaxpr/ppermute | solution.py:19
  183.9 9.3 %collective-permute-start = (bf16[16,4096]{1,0:T(8,128)(2,1)S(1)}, bf16[16,4096]{1,0:T(8,128)(2,1)S(1)}, u32[]{:S(2)}, u32[]{:S(2)}) collective-permute-start(bf16[16,4096]{1,0:T(8,128)(2,1)S(1)} %pad_maximum_fusion.7), channel_id=1, source_target_pairs={{16,0},{32,16},{48,32},{64,48},{80,64},{96,80},{112,96},{128,112},... | collective-permute-start | bytes 393224 | tf_op jit(solution)/shard_map/while/body/eval_jaxpr/ppermute | solution.py:19
  193.4 9.3 %collective-permute-start = (bf16[16,4096]{1,0:T(8,128)(2,1)S(1)}, bf16[16,4096]{1,0:T(8,128)(2,1)S(1)}, u32[]{:S(2)}, u32[]{:S(2)}) collective-permute-start(bf16[16,4096]{1,0:T(8,128)(2,1)S(1)} %pad_maximum_fusion.7), channel_id=1, source_target_pairs={{16,0},{32,16},{48,32},{64,48},{80,64},{96,80},{112,96},{128,112},... | collective-permute-start | bytes 393224 | tf_op jit(solution)/shard_map/while/body/eval_jaxpr/ppermute | solution.py:19
  202.8 9.3 %collective-permute-start = (bf16[16,4096]{1,0:T(8,128)(2,1)S(1)}, bf16[16,4096]{1,0:T(8,128)(2,1)S(1)}, u32[]{:S(2)}, u32[]{:S(2)}) collective-permute-start(bf16[16,4096]{1,0:T(8,128)(2,1)S(1)} %pad_maximum_fusion.7), channel_id=1, source_target_pairs={{16,0},{32,16},{48,32},{64,48},{80,64},{96,80},{112,96},{128,112},... | collective-permute-start | bytes 393224 | tf_op jit(solution)/shard_map/while/body/eval_jaxpr/ppermute | solution.py:19
  212.2 9.3 %collective-permute-start = (bf16[16,4096]{1,0:T(8,128)(2,1)S(1)}, bf16[16,4096]{1,0:T(8,128)(2,1)S(1)}, u32[]{:S(2)}, u32[]{:S(2)}) collective-permute-start(bf16[16,4096]{1,0:T(8,128)(2,1)S(1)} %pad_maximum_fusion.7), channel_id=1, source_target_pairs={{16,0},{32,16},{48,32},{64,48},{80,64},{96,80},{112,96},{128,112},... | collective-permute-start | bytes 393224 | tf_op jit(solution)/shard_map/while/body/eval_jaxpr/ppermute | solution.py:19
  221.7 9.3 %collective-permute-start = (bf16[16,4096]{1,0:T(8,128)(2,1)S(1)}, bf16[16,4096]{1,0:T(8,128)(2,1)S(1)}, u32[]{:S(2)}, u32[]{:S(2)}) collective-permute-start(bf16[16,4096]{1,0:T(8,128)(2,1)S(1)} %pad_maximum_fusion.7), channel_id=1, source_target_pairs={{16,0},{32,16},{48,32},{64,48},{80,64},{96,80},{112,96},{128,112},... | collective-permute-start | bytes 393224 | tf_op jit(solution)/shard_map/while/body/eval_jaxpr/ppermute | solution.py:19
  231.1 9.3 %collective-permute-start = (bf16[16,4096]{1,0:T(8,128)(2,1)S(1)}, bf16[16,4096]{1,0:T(8,128)(2,1)S(1)}, u32[]{:S(2)}, u32[]{:S(2)}) collective-permute-start(bf16[16,4096]{1,0:T(8,128)(2,1)S(1)} %pad_maximum_fusion.7), channel_id=1, source_target_pairs={{16,0},{32,16},{48,32},{64,48},{80,64},{96,80},{112,96},{128,112},... | collective-permute-start | bytes 393224 | tf_op jit(solution)/shard_map/while/body/eval_jaxpr/ppermute | solution.py:19
  240.5 9.3 %collective-permute-start = (bf16[16,4096]{1,0:T(8,128)(2,1)S(1)}, bf16[16,4096]{1,0:T(8,128)(2,1)S(1)}, u32[]{:S(2)}, u32[]{:S(2)}) collective-permute-start(bf16[16,4096]{1,0:T(8,128)(2,1)S(1)} %pad_maximum_fusion.7), channel_id=1, source_target_pairs={{16,0},{32,16},{48,32},{64,48},{80,64},{96,80},{112,96},{128,112},... | collective-permute-start | bytes 393224 | tf_op jit(solution)/shard_map/while/body/eval_jaxpr/ppermute | solution.py:19
  250.0 9.3 %collective-permute-start = (bf16[16,4096]{1,0:T(8,128)(2,1)S(1)}, bf16[16,4096]{1,0:T(8,128)(2,1)S(1)}, u32[]{:S(2)}, u32[]{:S(2)}) collective-permute-start(bf16[16,4096]{1,0:T(8,128)(2,1)S(1)} %pad_maximum_fusion.7), channel_id=1, source_target_pairs={{16,0},{32,16},{48,32},{64,48},{80,64},{96,80},{112,96},{128,112},... | collective-permute-start | bytes 393224 | tf_op jit(solution)/shard_map/while/body/eval_jaxpr/ppermute | solution.py:19
  259.4 9.3 %collective-permute-start = (bf16[16,4096]{1,0:T(8,128)(2,1)S(1)}, bf16[16,4096]{1,0:T(8,128)(2,1)S(1)}, u32[]{:S(2)}, u32[]{:S(2)}) collective-permute-start(bf16[16,4096]{1,0:T(8,128)(2,1)S(1)} %pad_maximum_fusion.7), channel_id=1, source_target_pairs={{16,0},{32,16},{48,32},{64,48},{80,64},{96,80},{112,96},{128,112},... | collective-permute-start | bytes 393224 | tf_op jit(solution)/shard_map/while/body/eval_jaxpr/ppermute | solution.py:19
  268.8 9.3 %collective-permute-start = (bf16[16,4096]{1,0:T(8,128)(2,1)S(1)}, bf16[16,4096]{1,0:T(8,128)(2,1)S(1)}, u32[]{:S(2)}, u32[]{:S(2)}) collective-permute-start(bf16[16,4096]{1,0:T(8,128)(2,1)S(1)} %pad_maximum_fusion.7), channel_id=1, source_target_pairs={{16,0},{32,16},{48,32},{64,48},{80,64},{96,80},{112,96},{128,112},... | collective-permute-start | bytes 393224 | tf_op jit(solution)/shard_map/while/body/eval_jaxpr/ppermute | solution.py:19
  306.5 78.3 %collective-permute-start = (bf16[16,4096]{1,0:T(8,128)(2,1)S(1)}, bf16[16,4096]{1,0:T(8,128)(2,1)S(1)}, u32[]{:S(2)}, u32[]{:S(2)}) collective-permute-start(bf16[16,4096]{1,0:T(8,128)(2,1)S(1)} %pad_maximum_fusion.7), channel_id=1, source_target_pairs={{16,0},{32,16},{48,32},{64,48},{80,64},{96,80},{112,96},{128,112},... | collective-permute-start | bytes 393224 | tf_op jit(solution)/shard_map/while/body/eval_jaxpr/ppermute | solution.py:19
  427.2 9.4 %collective-permute-start = (bf16[16,4096]{1,0:T(8,128)(2,1)S(1)}, bf16[16,4096]{1,0:T(8,128)(2,1)S(1)}, u32[]{:S(2)}, u32[]{:S(2)}) collective-permute-start(bf16[16,4096]{1,0:T(8,128)(2,1)S(1)} %pad_maximum_fusion.7), channel_id=1, source_target_pairs={{16,0},{32,16},{48,32},{64,48},{80,64},{96,80},{112,96},{128,112},... | collective-permute-start | bytes 393224 | tf_op jit(solution)/shard_map/while/body/eval_jaxpr/ppermute | solution.py:19
  479.0 9.4 %collective-permute-start = (bf16[16,4096]{1,0:T(8,128)(2,1)S(1)}, bf16[16,4096]{1,0:T(8,128)(2,1)S(1)}, u32[]{:S(2)}, u32[]{:S(2)}) collective-permute-start(bf16[16,4096]{1,0:T(8,128)(2,1)S(1)} %pad_maximum_fusion.7), channel_id=1, source_target_pairs={{16,0},{32,16},{48,32},{64,48},{80,64},{96,80},{112,96},{128,112},... | collective-permute-start | bytes 393224 | tf_op jit(solution)/shard_map/while/body/eval_jaxpr/ppermute | solution.py:19
  496.3 13.6 %collective-permute-start = (bf16[16,4096]{1,0:T(8,128)(2,1)S(1)}, bf16[16,4096]{1,0:T(8,128)(2,1)S(1)}, u32[]{:S(2)}, u32[]{:S(2)}) collective-permute-start(bf16[16,4096]{1,0:T(8,128)(2,1)S(1)} %pad_maximum_fusion.7), channel_id=1, source_target_pairs={{16,0},{32,16},{48,32},{64,48},{80,64},{96,80},{112,96},{128,112},... | collective-permute-start | bytes 393224 | tf_op jit(solution)/shard_map/while/body/eval_jaxpr/ppermute | solution.py:19
  523.7 17.3 %collective-permute-start = (bf16[16,4096]{1,0:T(8,128)(2,1)S(1)}, bf16[16,4096]{1,0:T(8,128)(2,1)S(1)}, u32[]{:S(2)}, u32[]{:S(2)}) collective-permute-start(bf16[16,4096]{1,0:T(8,128)(2,1)S(1)} %pad_maximum_fusion.7), channel_id=1, source_target_pairs={{16,0},{32,16},{48,32},{64,48},{80,64},{96,80},{112,96},{128,112},... | collective-permute-start | bytes 393224 | tf_op jit(solution)/shard_map/while/body/eval_jaxpr/ppermute | solution.py:19
  541.1 9.3 %collective-permute-start = (bf16[16,4096]{1,0:T(8,128)(2,1)S(1)}, bf16[16,4096]{1,0:T(8,128)(2,1)S(1)}, u32[]{:S(2)}, u32[]{:S(2)}) collective-permute-start(bf16[16,4096]{1,0:T(8,128)(2,1)S(1)} %pad_maximum_fusion.7), channel_id=1, source_target_pairs={{16,0},{32,16},{48,32},{64,48},{80,64},{96,80},{112,96},{128,112},... | collective-permute-start | bytes 393224 | tf_op jit(solution)/shard_map/while/body/eval_jaxpr/ppermute | solution.py:19
  550.6 9.3 %collective-permute-start = (bf16[16,4096]{1,0:T(8,128)(2,1)S(1)}, bf16[16,4096]{1,0:T(8,128)(2,1)S(1)}, u32[]{:S(2)}, u32[]{:S(2)}) collective-permute-start(bf16[16,4096]{1,0:T(8,128)(2,1)S(1)} %pad_maximum_fusion.7), channel_id=1, source_target_pairs={{16,0},{32,16},{48,32},{64,48},{80,64},{96,80},{112,96},{128,112},... | collective-permute-start | bytes 393224 | tf_op jit(solution)/shard_map/while/body/eval_jaxpr/ppermute | solution.py:19
  560.0 9.3 %collective-permute-start = (bf16[16,4096]{1,0:T(8,128)(2,1)S(1)}, bf16[16,4096]{1,0:T(8,128)(2,1)S(1)}, u32[]{:S(2)}, u32[]{:S(2)}) collective-permute-start(bf16[16,4096]{1,0:T(8,128)(2,1)S(1)} %pad_maximum_fusion.7), channel_id=1, source_target_pairs={{16,0},{32,16},{48,32},{64,48},{80,64},{96,80},{112,96},{128,112},... | collective-permute-start | bytes 393224 | tf_op jit(solution)/shard_map/while/body/eval_jaxpr/ppermute | solution.py:19
  569.5 9.3 %collective-permute-start = (bf16[16,4096]{1,0:T(8,128)(2,1)S(1)}, bf16[16,4096]{1,0:T(8,128)(2,1)S(1)}, u32[]{:S(2)}, u32[]{:S(2)}) collective-permute-start(bf16[16,4096]{1,0:T(8,128)(2,1)S(1)} %pad_maximum_fusion.7), channel_id=1, source_target_pairs={{16,0},{32,16},{48,32},{64,48},{80,64},{96,80},{112,96},{128,112},... | collective-permute-start | bytes 393224 | tf_op jit(solution)/shard_map/while/body/eval_jaxpr/ppermute | solution.py:19
  578.9 9.3 %collective-permute-start = (bf16[16,4096]{1,0:T(8,128)(2,1)S(1)}, bf16[16,4096]{1,0:T(8,128)(2,1)S(1)}, u32[]{:S(2)}, u32[]{:S(2)}) collective-permute-start(bf16[16,4096]{1,0:T(8,128)(2,1)S(1)} %pad_maximum_fusion.7), channel_id=1, source_target_pairs={{16,0},{32,16},{48,32},{64,48},{80,64},{96,80},{112,96},{128,112},... | collective-permute-start | bytes 393224 | tf_op jit(solution)/shard_map/while/body/eval_jaxpr/ppermute | solution.py:19
  588.3 9.3 %collective-permute-start = (bf16[16,4096]{1,0:T(8,128)(2,1)S(1)}, bf16[16,4096]{1,0:T(8,128)(2,1)S(1)}, u32[]{:S(2)}, u32[]{:S(2)}) collective-permute-start(bf16[16,4096]{1,0:T(8,128)(2,1)S(1)} %pad_maximum_fusion.7), channel_id=1, source_target_pairs={{16,0},{32,16},{48,32},{64,48},{80,64},{96,80},{112,96},{128,112},... | collective-permute-start | bytes 393224 | tf_op jit(solution)/shard_map/while/body/eval_jaxpr/ppermute | solution.py:19
  597.7 9.4 %collective-permute-start = (bf16[16,4096]{1,0:T(8,128)(2,1)S(1)}, bf16[16,4096]{1,0:T(8,128)(2,1)S(1)}, u32[]{:S(2)}, u32[]{:S(2)}) collective-permute-start(bf16[16,4096]{1,0:T(8,128)(2,1)S(1)} %pad_maximum_fusion.7), channel_id=1, source_target_pairs={{16,0},{32,16},{48,32},{64,48},{80,64},{96,80},{112,96},{128,112},... | collective-permute-start | bytes 393224 | tf_op jit(solution)/shard_map/while/body/eval_jaxpr/ppermute | solution.py:19
  (18 other events, 100.6 us)
Sparse Core Ops, SparseCore 0:
  10.6 83.8 all-gather.1
  617.7 94.5 reduce-scatter.3
where the time goes:
time: 724 us; the launch traced here: 722 us
  waiting for transfers between devices  356 us (49%)
  starting transfers between devices  230 us (32%)
  matrix products  35.7 us (5%)
  blocking collectives  33.1 us (5%)
  other arithmetic  33 us (5%)
  local copies, waits for them, and re-layouts  16.3 us (2%)
  between operations  14.1 us (2%)
    ppermute x39, starting transfers between devices, from_behind(): return lax.ppermute(array, axis, pairs)  230 us
    ppermute x39, waiting for transfers between devices, from_behind(): return lax.ppermute(array, axis, pairs)  209 us
    all_gather x1, waiting for transfers between devices, in_one_piece(): result = lax.all_gather(both, axis, axis=dim, tiled=True)  85.5 us
    unnamed x3, waiting for transfers between devices  61.7 us
    psum x1, blocking collectives, shards(): gain_total = lax.psum(gain_acc, 'dp')  33.1 us
    dot_general x8, matrix products, coupling_back(): jnp.dot(normed_second, w_second, preferred_element_type=jnp.float32)  18.3 us
  transfers between devices with their start and end apart: 41, of which 41 were waited for; matrix products, arithmetic and copies ran while one was open for 0% of the time, Pallas kernels for 0%

commit v1 on v0

v1 whole, which is shorter than its diff:
```python
import functools

import jax
import jax.numpy as jnp
from jax import lax
from jax.experimental import pallas as pl
from jax.experimental.pallas import tpu as pltpu
from jax.sharding import Mesh
from jax.sharding import PartitionSpec as P

offset = 0.25
CH = 1024
LAYERS = 8
ROWS = 16
F32, BF16 = jnp.float32, jnp.bfloat16


def silu_parts(pre):
    s = jax.nn.sigmoid(pre)
    return pre * s, s * (1.0 + pre * (1.0 - s))


def normalize(values, gain_row):
    inv = lax.rsqrt(jnp.mean(values * values, axis=-1, keepdims=True) + offset)
    return (values * inv * gain_row).astype(BF16), inv


def norm_back(values, inv, gain_row, upstream):
    weighted = gain_row * upstream
    return inv * weighted - values * (inv * inv * inv) * jnp.mean(
        weighted * values, axis=-1, keepdims=True
    )


def times(a, w):
    return jnp.dot(a, w, preferred_element_type=F32)


def times_transposed(a, w):
    return lax.dot_general(a, w, (((1,), (1,)), ((), ())), preferred_element_type=F32)


def layer_back(y1, y2, gy1, gy2, w_f, w_g, gain_f, gain_g):
    norm_g, inv_g = normalize(y1, gain_g)
    act_g, slope_g = silu_parts(times(norm_g, w_g()))
    x2 = y2 - act_g
    delta_g = (gy2 * slope_g).astype(BF16)
    norm_f, inv_f = normalize(x2, gain_f)
    act_f, slope_f = silu_parts(times(norm_f, w_f()))
    x1 = y1 - act_f
    back_g = times_transposed(delta_g, w_g())
    gz = gy1 + norm_back(y1, inv_g, gain_g, back_g)
    delta_f = (gz * slope_f).astype(BF16)
    back_f = times_transposed(delta_f, w_f())
    gx2 = gy2 + norm_back(x2, inv_f, gain_f, back_f)
    return x1, x2, gz, gx2, norm_f, delta_f, norm_g, delta_g, back_f, back_g, inv_f, inv_g


def stage_kernel(info, state, gains, own, other, bnd_in, bnd, out, wbuf, bbuf, wsem, bsem):
    del bnd_in

    def fetch(j, slot):
        layer = LAYERS - 1 - j
        row = (layer // 2) * CH
        mine = lax.rem(layer, 2) == info[1]

        @pl.when(mine)
        def _():
            pltpu.make_async_copy(own.at[pl.ds(row, CH)], wbuf.at[slot], wsem.at[slot]).start()

        @pl.when(jnp.logical_not(mine))
        def _():
            pltpu.make_async_copy(other.at[pl.ds(row, CH)], wbuf.at[slot], wsem.at[slot]).start()

    @pl.when(info[0] == 1)
    def _():
        fetch(0, 0)

        def step(j, carry):
            y1, y2, gy1, gy2 = carry
            slot = lax.rem(j, 2)
            layer = LAYERS - 1 - j
            bbuf[layer, :, 0:CH] = y1.astype(BF16)
            bbuf[layer, :, CH : 2 * CH] = y2.astype(BF16)
            bbuf[layer, :, 2 * CH : 3 * CH] = gy1.astype(BF16)
            bbuf[layer, :, 3 * CH : 4 * CH] = gy2.astype(BF16)
            pltpu.make_async_copy(own.at[pl.ds(0, CH)], wbuf.at[slot], wsem.at[slot]).wait()

            @pl.when(j < LAYERS - 1)
            def _():
                fetch(j + 1, 1 - slot)

            r = layer_back(
                y1,
                y2,
                gy1,
                gy2,
                lambda: wbuf[slot, :, 0:CH],
                lambda: wbuf[slot, :, CH : 2 * CH],
                gains[layer, 0:1, :],
                gains[layer, 1:2, :],
            )
            pltpu.make_async_copy(bbuf.at[layer], bnd.at[layer], bsem.at[layer]).start()
            return (r[0], r[1], r[2].astype(BF16).astype(F32), r[3].astype(BF16).astype(F32))

        first = tuple(state[:, k * CH : (k + 1) * CH].astype(F32) for k in range(4))
        last = lax.fori_loop(0, LAYERS, step, first)
        for k in range(4):
            out[:, k * CH : (k + 1) * CH] = last[k].astype(BF16)
        for k in range(LAYERS):
            pltpu.make_async_copy(bbuf.at[k], bnd.at[k], bsem.at[k]).wait()


def run_stage(info, state, gains, own, other, bnd):
    vmem = pl.BlockSpec(memory_space=pltpu.VMEM)
    hbm = pl.BlockSpec(memory_space=pl.ANY)
    return pl.pallas_call(
        stage_kernel,
        out_shape=(
            jax.ShapeDtypeStruct((LAYERS, ROWS, 4 * CH), BF16),
            jax.ShapeDtypeStruct((ROWS, 4 * CH), BF16),
        ),
        in_specs=[pl.BlockSpec(memory_space=pltpu.SMEM), vmem, vmem, hbm, hbm, hbm],
        out_specs=(hbm, vmem),
        scratch_shapes=[
            pltpu.VMEM((2, CH, 2 * CH), BF16),
            pltpu.VMEM((LAYERS, ROWS, 4 * CH), BF16),
            pltpu.SemaphoreType.DMA((2,)),
            pltpu.SemaphoreType.DMA((LAYERS,)),
        ],
        input_output_aliases={5: 0},
        compiler_params=pltpu.CompilerParams(vmem_limit_bytes=28 * 2**20),
        cost_estimate=pl.CostEstimate(
            flops=8 * 8 * ROWS * CH * CH, bytes_accessed=32 * 2**20, transcendentals=0
        ),
        name="stage",
    )(info, state, gains, own, other, bnd)


def owner_kernel(info, b, gains, own, pair, grad, parts, gain_sums, wbuf, wsem):
    copy = pltpu.make_async_copy(own.at[pl.ds(info[0] * CH, CH)], wbuf, wsem)
    copy.start()
    copy.wait()
    y1, y2, gy1, gy2 = (b[:, k * CH : (k + 1) * CH].astype(F32) for k in range(4))
    r = layer_back(
        y1,
        y2,
        gy1,
        gy2,
        lambda: wbuf[:, 0:CH],
        lambda: wbuf[:, CH : 2 * CH],
        gains[0:1, :],
        gains[1:2, :],
    )
    x1, x2, gz, gx2, norm_f, delta_f, norm_g, delta_g, back_f, back_g, inv_f, inv_g = r
    pair[:, 0:CH] = x1
    pair[:, CH : 2 * CH] = x2
    grad[:, 0:CH] = gz.astype(BF16)
    grad[:, CH : 2 * CH] = gx2.astype(BF16)
    gain_sums[0:1, :] = jnp.sum(back_f * x2 * inv_f, axis=0, keepdims=True)
    gain_sums[1:2, :] = jnp.sum(back_g * y1 * inv_g, axis=0, keepdims=True)
    contract = (((0,), (0,)), ((), ()))
    for at, n, d in ((0, norm_f, delta_f), (CH, norm_g, delta_g)):
        for k in range(0, CH, 256):
            part = lax.dot_general(n[:, k : k + 256], d, contract, preferred_element_type=F32)
            parts[k : k + 256, at : at + CH] = part.astype(BF16)


def run_owner(info, b, gains, own):
    vmem = pl.BlockSpec(memory_space=pltpu.VMEM)
    rows = b.shape[0]
    return pl.pallas_call(
        owner_kernel,
        out_shape=(
            jax.ShapeDtypeStruct((rows, 2 * CH), F32),
            jax.ShapeDtypeStruct((rows, 2 * CH), BF16),
            jax.ShapeDtypeStruct((CH, 2 * CH), BF16),
            jax.ShapeDtypeStruct((2, CH), F32),
        ),
        in_specs=[pl.BlockSpec(memory_space=pltpu.SMEM), vmem, vmem, pl.BlockSpec(memory_space=pl.ANY)],
        out_specs=(vmem, vmem, vmem, vmem),
        scratch_shapes=[pltpu.VMEM((CH, 2 * CH), BF16), pltpu.SemaphoreType.DMA],
        compiler_params=pltpu.CompilerParams(vmem_limit_bytes=48 * 2**20),
        cost_estimate=pl.CostEstimate(
            flops=12 * rows * CH * CH, bytes_accessed=12 * 2**20, transcendentals=0
        ),
        name="owner",
    )(info, b, gains, own)


def shards(out_pair, out_grad, f_weight, g_weight, gains):
    x, yh, c = (lax.axis_index(a) for a in ("x", "yh", "c"))
    shard = jnp.concatenate([f_weight[0], g_weight[0]], axis=1)
    own = lax.all_gather(shard, ("yh", "yl", "z"), axis=0, tiled=True)
    other = lax.ppermute(own, "c", [(0, 1), (1, 0)])
    all_gains = lax.all_gather(gains[0], ("yh", "c"), axis=0, tiled=False)
    at = (yh * 2 + c) * ROWS
    state = jnp.concatenate(
        [
            lax.dynamic_slice_in_dim(out_pair, at, ROWS, 0).astype(BF16),
            lax.dynamic_slice_in_dim(out_grad, at, ROWS, 0),
        ],
        axis=1,
    )
    bnd = jnp.zeros((LAYERS, ROWS, 4 * CH), BF16)
    for stage in range(4):
        info = jnp.stack([(x == 3 - stage).astype(jnp.int32), c.astype(jnp.int32)])
        bnd, out = run_stage(info, state, all_gains, own, other, bnd)
        if stage < 3:
            state = lax.ppermute(out, "x", [(3 - stage, 2 - stage)])
    mine = lax.all_to_all(bnd, ("yh", "c"), split_axis=0, concat_axis=0, tiled=True)
    mine = mine.reshape(LAYERS * ROWS, 4 * CH)
    info = jnp.reshape(yh, (1,)).astype(jnp.int32)
    pair, grad, parts, gain_part = run_owner(info, mine, gains[0], own)
    sums = lax.psum_scatter(parts, ("yl", "z"), scatter_dimension=0, tiled=True).astype(F32)
    gain_total = lax.psum(gain_part, ("yl", "z"))
    return (pair[None], grad[None], sums[None, :, :CH], sums[None, :, CH:], gain_total[None])


def solution(mesh):
    devices = mesh.devices.reshape(4, 4, 2, 2, 8)
    fine = Mesh(devices, ("x", "yh", "c", "yl", "z"))
    section, dp = ("x", "yh", "c"), ("yl", "z")
    return jax.shard_map(
        shards,
        mesh=fine,
        in_specs=(P(dp, None), P(dp, None), P(section, dp, None), P(section, dp, None), P(section, None, None)),
        out_specs=(
            P(section, dp, None),
            P(section, dp, None),
            P(section, dp, None),
            P(section, dp, None),
            P(section, None, None),
        ),
        check_vma=False,
    )
```

time: 724 us -> 457 us (0.63)
  starting transfers between devices: 230 us -> 5.25 us
  waiting for transfers between devices: 356 us -> 272 us
  blocking collectives: 33.1 us -> 103 us
  matrix products: 35.7 us -> 0 us
  Pallas kernels: 0 us -> 32.1 us
  other arithmetic: 33 us -> 2.99 us
  local copies, waits for them, and re-layouts: 16.3 us -> 26.9 us
    ppermute x39 -> x4, starting transfers between devices: 230 us -> 5.17 us  [the longest x3 3.26 us: shards(): state = lax.ppermute(out, 'x', [(3 - stage, 2 - stage)])]
    ppermute x39 -> x4, waiting for transfers between devices: 209 us -> 56.9 us  [the longest x3 56.9 us: shards(): state = lax.ppermute(out, 'x', [(3 - stage, 2 - stage)])]
    reduce_scatter x0 -> x1, waiting for transfers between devices: none -> 67.9 us  [shards(): lax.psum_scatter(parts, ('yl', 'z'), scatter_dimension=0, tiled=True)]
    unnamed x3 -> x2, waiting for transfers between devices: 61.7 us -> 0.03 us
    all_gather x1, waiting for transfers between devices: 85.5 us -> 147 us  [shards(): own = lax.all_gather(shard, ('yh', 'yl', 'z'), axis=0, tiled=True)]
    dot_general x34 -> x0, matrix products: 35.7 us -> none  [the longest x8 18.3 us: coupling_back(): jnp.dot(normed_second, w_second, preferred_element_type=jnp.float32)]
    all_gather x0 -> x1, blocking collectives: none -> 35.6 us  [shards(): all_gains = lax.all_gather(gains[0], ('yh', 'c'), axis=0, tiled=False)]
    all_to_all x0 -> x1, blocking collectives: none -> 33.5 us  [shards(): lax.all_to_all(bnd, ('yh', 'c'), split_axis=0, concat_axis=0, tiled=True)]
  transfers between devices with their start and end apart: 41 -> 6, of which waited for: 41 -> 4; matrix products, arithmetic and copies ran while one was open for 0% -> 0% of each run, Pallas kernels for 0% -> 0%
where the time goes in v1:
time: 457 us; the launch traced here: 456 us
  waiting for transfers between devices  272 us (60%)
  blocking collectives  103 us (23%)
  Pallas kernels  32.1 us (7%)
  local copies, waits for them, and re-layouts  26.9 us (6%)
  between operations  14.2 us (3%)
  starting transfers between devices  5.25 us (1%)
    all_gather x1, waiting for transfers between devices, shards(): own = lax.all_gather(shard, ('yh', 'yl', 'z'), axis=0, tiled=True)  147 us
    reduce_scatter x1, waiting for transfers between devices, shards(): lax.psum_scatter(parts, ('yl', 'z'), scatter_dimension=0, tiled=True)  67.9 us
    ppermute x3, waiting for transfers between devices, shards(): state = lax.ppermute(out, 'x', [(3 - stage, 2 - stage)])  56.9 us
    all_gather x1, blocking collectives, shards(): all_gains = lax.all_gather(gains[0], ('yh', 'c'), axis=0, tiled=False)  35.6 us
    psum x1, blocking collectives, shards(): gain_total = lax.psum(gain_part, ('yl', 'z'))  33.8 us
    all_to_all x1, blocking collectives, shards(): lax.all_to_all(bnd, ('yh', 'c'), split_axis=0, concat_axis=0, tiled=True)  33.5 us
    pallas_call x4, Pallas kernels, run_stage(): pl.pallas_call(stage_kernel, out_shape=(jax.ShapeDtypeStruct((LAYERS, ROW...  26 us
    unnamed x12, local copies, waits for them, and re-layouts  25 us
  transfers between devices with their start and end apart: 6, of which 4 were waited for; matrix products, arithmetic and copies ran while one was open for 0% of the time, Pallas kernels for 0%

profile of v1, /device:TPU:2, one launch (start us, length us, event | category | flops | bytes accessed | tf_op | source)
XLA Modules:
  0.0 456.1 jit_solution(4982940880083586982)
XLA Ops:
  7.2 0.0 all-gather.2.cloned.1.call-start
  7.2 1.7 pad_maximum_fusion
  8.9 0.0 reduce-scatter.2.cloned.1.call-start
  9.0 147.0 %all-gather.2.cloned.1.call-done.own = bf16[4096,2048]{1,0:T(8,128)(2,1)} async-done(((bf16[64,2048]{1,0:T(8,128)(2,1)}), bf16[4096,2048]{1,0:T(8,128)(2,1)}) %all-gather.2.cloned.1.call-update) | async-done | bytes 16777232 | tf_op jit(solution)/shard_map/all_gather | solution.py:194
  156.0 1.9 collective-permute-start
  157.9 35.6 %all_gather.6.gains = f32[8,2,1024]{2,1,0:T(2,128)S(1)} all-gather(f32[1,2,1024]{2,1,0:T(2,128)} %param.9), channel_id=1, replica_groups=mesh['x'=4,'yh'=4,'c'=2,'yl'=2,'z'=8] {'yh','c'}, dimensions={0}, use_global_device_ids=true | all-gather | bytes 73728 | tf_op jit(solution)/shard_map/all_gather | solution.py:196
  193.5 0.1 pad_add_fusion.3.info
  193.5 0.9 dynamic-slice_convert_fusion
  194.5 0.1 broadcast_in_dim.18.bnd_in
  194.6 5.8 %copy-done = bf16[4096,2048]{1,0:T(8,128)(2,1)S(1)} copy-done((bf16[4096,2048]{1,0:T(8,128)(2,1)S(1)}, bf16[4096,2048]{1,0:T(8,128)(2,1)}, u32[]{:S(2)}) %copy-start) | copy-done | bytes 16777240
  200.4 0.6 stage.4
  201.0 0.7 collective-permute-start.1
  201.7 0.1 pad_add_fusion.2.info
  201.8 5.8 %copy-done.1 = bf16[4096,2048]{1,0:T(8,128)(2,1)S(1)} copy-done((bf16[4096,2048]{1,0:T(8,128)(2,1)S(1)}, bf16[4096,2048]{1,0:T(8,128)(2,1)}, u32[]{:S(2)}) %copy-start.1) | copy-done | bytes 16777240
  207.5 0.6 stage.5
  208.2 1.3 collective-permute-start.2
  209.5 0.1 pad_add_fusion.1.info
  209.6 54.5 %collective-permute-done.2.state = bf16[16,4096]{1,0:T(8,128)(2,1)S(1)} collective-permute-done((bf16[16,4096]{1,0:T(8,128)(2,1)S(1)}, bf16[16,4096]{1,0:T(8,128)(2,1)S(1)}, u32[]{:S(2)}, u32[]{:S(2)}) %collective-permute-start.2) | collective-permute-done | bytes 131104 | tf_op jit(solution)/shard_map/ppermute | solution.py:210
  264.0 5.8 %copy-done.2 = bf16[4096,2048]{1,0:T(8,128)(2,1)S(1)} copy-done((bf16[4096,2048]{1,0:T(8,128)(2,1)S(1)}, bf16[4096,2048]{1,0:T(8,128)(2,1)}, u32[]{:S(2)}) %copy-start.2) | copy-done | bytes 16777240
  269.8 23.4 %stage.6 = (bf16[8,16,4096]{2,1,0:T(8,128)(2,1)S(1)}, bf16[16,4096]{1,0:T(8,128)(2,1)S(1)}) custom-call(s32[2]{0:T(128)S(1)} %pad_add_fusion.1.info, bf16[16,4096]{1,0:T(8,128)(2,1)S(1)} %collective-permute-done.2.state, f32[8,2,1024]{2,1,0:T(2,128)S(1)} %all_gather.6.gains, bf16[4096,2048]{1,0:T(8,128)(2,1)S(1)} %copy-done.2, ...), custom_call_target="tpu_custom_call", output_to_operand_aliasing={{0}: (5, {})} | custom-call | flops 1073741824 | bytes 33554432 | tf_op jit(solution)/shard_map/stage/pallas_call | solution.py:117
  293.2 1.3 collective-permute-start.3
  294.5 0.1 pad_add_fusion.info
  294.6 2.4 collective-permute-done.3.state
  297.0 5.8 %copy-done.3 = bf16[4096,2048]{1,0:T(8,128)(2,1)S(1)} copy-done((bf16[4096,2048]{1,0:T(8,128)(2,1)S(1)}, bf16[4096,2048]{1,0:T(8,128)(2,1)}, u32[]{:S(2)}) %copy-start.3) | copy-done | bytes 16777240
  302.8 1.3 stage.7
  304.1 33.5 %all_to_all.5 = bf16[8,16,4096]{2,1,0:T(8,128)(2,1)S(1)} all-to-all(bf16[8,16,4096]{2,1,0:T(8,128)(2,1)S(1)} %get-tuple-element.22), channel_id=1, replica_groups=mesh['x'=4,'yh'=4,'c'=2,'yl'=2,'z'=8] {'yh','c'}, dimensions={0} | all-to-all | bytes 2097152 | tf_op jit(solution)/shard_map/all_to_all | solution.py:211
  337.6 6.1 %owner.1 = (f32[128,2048]{1,0:T(8,128)}, bf16[128,2048]{1,0:T(8,128)(2,1)}, bf16[1024,2048]{1,0:T(8,128)(2,1)S(1)}, f32[2,1024]{1,0:T(2,128)S(1)}) custom-call(s32[1]{0:T(128)} %bitcast.info, bf16[128,4096]{1,0:T(8,128)(2,1)S(1)} %bitcast.17, f32[2,1024]{1,0:T(2,128)S(1)} %bitcast.18, bf16[4096,2048]{1,0:T(8,128)(2,1)} %all-gather.2.cloned.1.call-done.own), custom_call_target="tpu_custom_call" | custom-call | flops 1610612736 | bytes 12582912 | tf_op jit(solution)/shard_map/owner/pallas_call | solution.py:172
  343.7 2.0 copy-done.4
  345.7 33.8 %psum.7 = f32[1,2,1024]{2,1,0:T(2,128)} all-reduce(f32[1,2,1024]{2,1,0:T(2,128)S(1)} %bitcast.19), channel_id=1, replica_groups=mesh['x'=4,'yh'=4,'c'=2,'yl'=2,'z'=8] {'yl','z'}, use_global_device_ids=true, to_apply=%region_1.0 | all-reduce | flops 2048 | bytes 16384 | tf_op jit(solution)/shard_map/psum | solution.py:216
  379.5 67.9 %reduce-scatter.2.cloned.1.call-done = bf16[64,2048]{1,0:T(8,128)(2,1)} async-done(((bf16[1024,2048]{1,0:T(8,128)(2,1)}), bf16[64,2048]{1,0:T(8,128)(2,1)}) %reduce-scatter.2.cloned.1.call-update) | async-done | bytes 262160 | tf_op jit(solution)/shard_map/reduce_scatter | solution.py:215
  447.4 1.0 convert_element_type.5
  448.4 0.8 slice_bitcast_fusion
  (12 shorter events, 0.1 us)
Async XLA Ops:
  7.2 148.8 %all-gather.2.cloned.1.call-start = ((), (), s32[]{:S(2)}) async-start(), calls=%async_computation.2 | async-start | bytes 17039360 | tf_op jit(solution)/shard_map/all_gather | solution.py:194
  8.9 438.5 %reduce-scatter.2.cloned.1.call-start = ((), (), s32[]{:S(2)}) async-start(), calls=%async_computation.3 | async-start | bytes 4456448 | tf_op jit(solution)/shard_map/reduce_scatter | solution.py:215
  156.0 38.5 %collective-permute-start = (bf16[4096,2048]{1,0:T(8,128)(2,1)}, bf16[4096,2048]{1,0:T(8,128)(2,1)}, u32[]{:S(2)}, u32[]{:S(2)}) collective-permute-start(bf16[4096,2048]{1,0:T(8,128)(2,1)} %all-gather.2.cloned.1.call-done.own), channel_id=1, source_target_pairs={{0,16},{16,0},{1,17},{17,1},{2,18},{18,2},{3,19},{19,3},{4,20},{20... | collective-permute-start | bytes 50331656 | tf_op jit(solution)/shard_map/ppermute | solution.py:195
  194.6 5.8 %copy-start = (bf16[4096,2048]{1,0:T(8,128)(2,1)S(1)}, bf16[4096,2048]{1,0:T(8,128)(2,1)}, u32[]{:S(2)}) copy-start(bf16[4096,2048]{1,0:T(8,128)(2,1)} %all-gather.2.cloned.1.call-done.own) | copy-start | bytes 50331652
  201.0 0.8 collective-permute-start.1
  201.8 5.8 %copy-start.1 = (bf16[4096,2048]{1,0:T(8,128)(2,1)S(1)}, bf16[4096,2048]{1,0:T(8,128)(2,1)}, u32[]{:S(2)}) copy-start(bf16[4096,2048]{1,0:T(8,128)(2,1)} %all-gather.2.cloned.1.call-done.own) | copy-start | bytes 50331652
  208.2 55.9 %collective-permute-start.2 = (bf16[16,4096]{1,0:T(8,128)(2,1)S(1)}, bf16[16,4096]{1,0:T(8,128)(2,1)S(1)}, u32[]{:S(2)}, u32[]{:S(2)}) collective-permute-start(bf16[16,4096]{1,0:T(8,128)(2,1)S(1)} %get-tuple-element.18), channel_id=1, source_target_pairs={{256,128},{257,129},{258,130},{259,131},{260,132},{261,133},{262,1... | collective-permute-start | bytes 393224 | tf_op jit(solution)/shard_map/ppermute | solution.py:210
  264.0 5.8 %copy-start.2 = (bf16[4096,2048]{1,0:T(8,128)(2,1)S(1)}, bf16[4096,2048]{1,0:T(8,128)(2,1)}, u32[]{:S(2)}) copy-start(bf16[4096,2048]{1,0:T(8,128)(2,1)} %all-gather.2.cloned.1.call-done.own) | copy-start | bytes 50331652
  293.2 3.8 collective-permute-start.3
  297.0 5.8 %copy-start.3 = (bf16[4096,2048]{1,0:T(8,128)(2,1)S(1)}, bf16[4096,2048]{1,0:T(8,128)(2,1)}, u32[]{:S(2)}) copy-start(bf16[4096,2048]{1,0:T(8,128)(2,1)} %all-gather.2.cloned.1.call-done.own) | copy-start | bytes 50331652
  302.8 34.8 %copy-start.5 = (f32[1,2,1024]{2,1,0:T(2,128)S(1)}, f32[1,2,1024]{2,1,0:T(2,128)}, u32[]{:S(2)}) copy-start(f32[1,2,1024]{2,1,0:T(2,128)} %param.9) | copy-start | bytes 24580
  343.7 2.0 copy-start.4
Sparse Core Ops, SparseCore 0:
  11.6 144.3 all-gather.1
  345.8 101.5 reduce-scatter.1

commit v2 on v1

--- a/solution.py
+++ b/solution.py
@@ -40,20 +40,23 @@
     return lax.dot_general(a, w, (((1,), (1,)), ((), ())), preferred_element_type=F32)
 
 
-def layer_back(y1, y2, gy1, gy2, w_f, w_g, gain_f, gain_g):
+def pair_back(y1, y2, w_f, w_g, gain_f, gain_g):
     norm_g, inv_g = normalize(y1, gain_g)
-    act_g, slope_g = silu_parts(times(norm_g, w_g()))
+    act_g, slope_g = silu_parts(times(norm_g, w_g))
     x2 = y2 - act_g
+    norm_f, inv_f = normalize(x2, gain_f)
+    act_f, slope_f = silu_parts(times(norm_f, w_f))
+    return y1 - act_f, x2, slope_f, slope_g, inv_f, inv_g, norm_f, norm_g
+
+
+def grad_back(gy1, gy2, y1, x2, slope_f, slope_g, inv_f, inv_g, w_f, w_g, gain_f, gain_g):
     delta_g = (gy2 * slope_g).astype(BF16)
-    norm_f, inv_f = normalize(x2, gain_f)
-    act_f, slope_f = silu_parts(times(norm_f, w_f()))
-    x1 = y1 - act_f
-    back_g = times_transposed(delta_g, w_g())
+    back_g = times_transposed(delta_g, w_g)
     gz = gy1 + norm_back(y1, inv_g, gain_g, back_g)
     delta_f = (gz * slope_f).astype(BF16)
-    back_f = times_transposed(delta_f, w_f())
+    back_f = times_transposed(delta_f, w_f)
     gx2 = gy2 + norm_back(x2, inv_f, gain_f, back_f)
-    return x1, x2, gz, gx2, norm_f, delta_f, norm_g, delta_g, back_f, back_g, inv_f, inv_g
+    return gz, gx2, delta_f, delta_g, back_f, back_g
 
 
 def stage_kernel(info, state, gains, own, other, bnd_in, bnd, out, wbuf, bbuf, wsem, bsem):
@@ -72,48 +75,62 @@
         def _():
             pltpu.make_async_copy(other.at[pl.ds(row, CH)], wbuf.at[slot], wsem.at[slot]).start()
 
+    def gain_rows(j):
+        layer = LAYERS - 1 - j
+        far = lax.rem(info[2] - layer // 2 + 4, 4)
+        part = lax.rem(layer, 2)
+        return gains[far, part, 0:1, :], gains[far, part, 1:2, :]
+
+    def weights(j):
+        slot = lax.rem(j, 3)
+        return wbuf[slot, :, 0:CH], wbuf[slot, :, CH : 2 * CH]
+
+    def pairs(j, y1, y2):
+        slot = lax.rem(j, 3)
+        layer = LAYERS - 1 - j
+        bbuf[layer, :, 0:CH] = y1.astype(BF16)
+        bbuf[layer, :, CH : 2 * CH] = y2.astype(BF16)
+        pltpu.make_async_copy(own.at[pl.ds(0, CH)], wbuf.at[slot], wsem.at[slot]).wait()
+        r = pair_back(y1, y2, *weights(j), *gain_rows(j))
+        return r[0], r[1], (y1,) + r[1:6]
+
+    def grads(j, gy1, gy2, kept):
+        layer = LAYERS - 1 - j
+        bbuf[layer, :, 2 * CH : 3 * CH] = gy1.astype(BF16)
+        bbuf[layer, :, 3 * CH : 4 * CH] = gy2.astype(BF16)
+        r = grad_back(gy1, gy2, *kept, *weights(j), *gain_rows(j))
+        return r[0].astype(BF16).astype(F32), r[1].astype(BF16).astype(F32)
+
     @pl.when(info[0] == 1)
     def _():
         fetch(0, 0)
+        fetch(1, 1)
+        y1, y2, gy1, gy2 = (state[:, k * CH : (k + 1) * CH].astype(F32) for k in range(4))
+        x1, x2, kept = pairs(0, y1, y2)
 
         def step(j, carry):
-            y1, y2, gy1, gy2 = carry
-            slot = lax.rem(j, 2)
-            layer = LAYERS - 1 - j
-            bbuf[layer, :, 0:CH] = y1.astype(BF16)
-            bbuf[layer, :, CH : 2 * CH] = y2.astype(BF16)
-            bbuf[layer, :, 2 * CH : 3 * CH] = gy1.astype(BF16)
-            bbuf[layer, :, 3 * CH : 4 * CH] = gy2.astype(BF16)
-            pltpu.make_async_copy(own.at[pl.ds(0, CH)], wbuf.at[slot], wsem.at[slot]).wait()
+            y1, y2, gy1, gy2, kept = carry
 
             @pl.when(j < LAYERS - 1)
             def _():
-                fetch(j + 1, 1 - slot)
-
-            r = layer_back(
-                y1,
-                y2,
-                gy1,
-                gy2,
-                lambda: wbuf[slot, :, 0:CH],
-                lambda: wbuf[slot, :, CH : 2 * CH],
-                gains[layer, 0:1, :],
-                gains[layer, 1:2, :],
-            )
-            pltpu.make_async_copy(bbuf.at[layer], bnd.at[layer], bsem.at[layer]).start()
-            return (r[0], r[1], r[2].astype(BF16).astype(F32), r[3].astype(BF16).astype(F32))
-
-        first = tuple(state[:, k * CH : (k + 1) * CH].astype(F32) for k in range(4))
-        last = lax.fori_loop(0, LAYERS, step, first)
-        for k in range(4):
-            out[:, k * CH : (k + 1) * CH] = last[k].astype(BF16)
-        for k in range(LAYERS):
-            pltpu.make_async_copy(bbuf.at[k], bnd.at[k], bsem.at[k]).wait()
+                fetch(j + 1, lax.rem(j + 1, 3))
+
+            x1, x2, fresh = pairs(j, y1, y2)
+            gz, gx2 = grads(j - 1, gy1, gy2, kept)
+            return x1, x2, gz, gx2, fresh
+
+        x1, x2, gy1, gy2, kept = lax.fori_loop(1, LAYERS, step, (x1, x2, gy1, gy2, kept))
+        gz, gx2 = grads(LAYERS - 1, gy1, gy2, kept)
+        for k, v in enumerate((x1, x2, gz, gx2)):
+            out[:, k * CH : (k + 1) * CH] = v.astype(BF16)
+        copy = pltpu.make_async_copy(bbuf, bnd, bsem)
+        copy.start()
+        copy.wait()
 
 
 def run_stage(info, state, gains, own, other, bnd):
     vmem = pl.BlockSpec(memory_space=pltpu.VMEM)
-    hbm = pl.BlockSpec(memory_space=pl.ANY)
+    hbm = pl.BlockSpec(memory_space=pltpu.HBM)
     return pl.pallas_call(
         stage_kernel,
         out_shape=(
@@ -123,13 +140,13 @@
         in_specs=[pl.BlockSpec(memory_space=pltpu.SMEM), vmem, vmem, hbm, hbm, hbm],
         out_specs=(hbm, vmem),
         scratch_shapes=[
-            pltpu.VMEM((2, CH, 2 * CH), BF16),
+            pltpu.VMEM((3, CH, 2 * CH), BF16),
             pltpu.VMEM((LAYERS, ROWS, 4 * CH), BF16),
-            pltpu.SemaphoreType.DMA((2,)),
-            pltpu.SemaphoreType.DMA((LAYERS,)),
+            pltpu.SemaphoreType.DMA((3,)),
+            pltpu.SemaphoreType.DMA,
         ],
         input_output_aliases={5: 0},
-        compiler_params=pltpu.CompilerParams(vmem_limit_bytes=28 * 2**20),
+        compiler_params=pltpu.CompilerParams(vmem_limit_bytes=56 * 2**20),
         cost_estimate=pl.CostEstimate(
             flops=8 * 8 * ROWS * CH * CH, bytes_accessed=32 * 2**20, transcendentals=0
         ),
@@ -142,17 +159,12 @@
     copy.start()
     copy.wait()
     y1, y2, gy1, gy2 = (b[:, k * CH : (k + 1) * CH].astype(F32) for k in range(4))
-    r = layer_back(
-        y1,
-        y2,
-        gy1,
-        gy2,
-        lambda: wbuf[:, 0:CH],
-        lambda: wbuf[:, CH : 2 * CH],
-        gains[0:1, :],
-        gains[1:2, :],
-    )
-    x1, x2, gz, gx2, norm_f, delta_f, norm_g, delta_g, back_f, back_g, inv_f, inv_g = r
+    w_f, w_g = wbuf[:, 0:CH], wbuf[:, CH : 2 * CH]
+    gain_f, gain_g = gains[0:1, :], gains[1:2, :]
+    x1, x2, slope_f, slope_g, inv_f, inv_g, norm_f, norm_g = pair_back(y1, y2, w_f, w_g, gain_f, gain_g)
+    gz, gx2, delta_f, delta_g, back_f, back_g = grad_back(
+        gy1, gy2, y1, x2, slope_f, slope_g, inv_f, inv_g, w_f, w_g, gain_f, gain_g
+    )
     pair[:, 0:CH] = x1
     pair[:, CH : 2 * CH] = x2
     grad[:, 0:CH] = gz.astype(BF16)
@@ -177,10 +189,10 @@
             jax.ShapeDtypeStruct((CH, 2 * CH), BF16),
             jax.ShapeDtypeStruct((2, CH), F32),
         ),
-        in_specs=[pl.BlockSpec(memory_space=pltpu.SMEM), vmem, vmem, pl.BlockSpec(memory_space=pl.ANY)],
+        in_specs=[pl.BlockSpec(memory_space=pltpu.SMEM), vmem, vmem, pl.BlockSpec(memory_space=pltpu.HBM)],
         out_specs=(vmem, vmem, vmem, vmem),
         scratch_shapes=[pltpu.VMEM((CH, 2 * CH), BF16), pltpu.SemaphoreType.DMA],
-        compiler_params=pltpu.CompilerParams(vmem_limit_bytes=48 * 2**20),
+        compiler_params=pltpu.CompilerParams(vmem_limit_bytes=52 * 2**20),
         cost_estimate=pl.CostEstimate(
             flops=12 * rows * CH * CH, bytes_accessed=12 * 2**20, transcendentals=0
         ),
@@ -193,7 +205,12 @@
     shard = jnp.concatenate([f_weight[0], g_weight[0]], axis=1)
     own = lax.all_gather(shard, ("yh", "yl", "z"), axis=0, tiled=True)
     other = lax.ppermute(own, "c", [(0, 1), (1, 0)])
-    all_gains = lax.all_gather(gains[0], ("yh", "c"), axis=0, tiled=False)
+    swapped = lax.ppermute(gains[0], "c", [(0, 1), (1, 0)])
+    chip_gains = jnp.where(c == 0, jnp.stack([gains[0], swapped]), jnp.stack([swapped, gains[0]]))
+    far_gains = [
+        lax.ppermute(chip_gains, "yh", [(i, (i + by) % 4) for i in range(4)]) for by in (1, 2, 3)
+    ]
+    all_gains = jnp.stack([chip_gains] + far_gains)
     at = (yh * 2 + c) * ROWS
     state = jnp.concatenate(
         [
@@ -204,7 +221,7 @@
     )
     bnd = jnp.zeros((LAYERS, ROWS, 4 * CH), BF16)
     for stage in range(4):
-        info = jnp.stack([(x == 3 - stage).astype(jnp.int32), c.astype(jnp.int32)])
+        info = jnp.stack([(x == 3 - stage).astype(jnp.int32), c.astype(jnp.int32), yh.astype(jnp.int32)])
         bnd, out = run_stage(info, state, all_gains, own, other, bnd)
         if stage < 3:
             state = lax.ppermute(out, "x", [(3 - stage, 2 - stage)])

time: 457 us -> 445 us (0.974)
  the two profiles are of different devices: /device:TPU:2 before, /device:TPU:4 now
where the time goes in v2:
time: 445 us; the launch traced here: 444 us
  waiting for transfers between devices  289 us (65%)
  blocking collectives  68.3 us (15%)
  Pallas kernels  36.4 us (8%)
  starting transfers between devices  23 us (5%)
  between operations  14.2 us (3%)
  other arithmetic  7.94 us (2%)
  local copies, waits for them, and re-layouts  4.79 us (1%)
    all_gather x1, waiting for transfers between devices, shards(): own = lax.all_gather(shard, ('yh', 'yl', 'z'), axis=0, tiled=True)  147 us
    reduce_scatter x1, waiting for transfers between devices, shards(): lax.psum_scatter(parts, ('yl', 'z'), scatter_dimension=0, tiled=True)  93.2 us
    all_to_all x1, blocking collectives, shards(): lax.all_to_all(bnd, ('yh', 'c'), split_axis=0, concat_axis=0, tiled=True)  34.7 us
    psum x1, blocking collectives, shards(): gain_total = lax.psum(gain_part, ('yl', 'z'))  33.7 us
    pallas_call x4, Pallas kernels, run_stage(): pl.pallas_call(stage_kernel, out_shape=(jax.ShapeDtypeStruct((LAYERS, ROW...  28.4 us
    ppermute x3, waiting for transfers between devices, shards(): state = lax.ppermute(out, 'x', [(3 - stage, 2 - stage)])  27.7 us
    ppermute x1, waiting for transfers between devices, shards(): swapped = lax.ppermute(gains[0], 'c', [(0, 1), (1, 0)])  20.8 us
    ppermute x3, starting transfers between devices, shards(): lax.ppermute(chip_gains, 'yh', [(i, (i + by) % 4) for i in range(4)])  15.3 us
  transfers between devices with their start and end apart: 10, of which 6 were waited for; matrix products, arithmetic and copies ran while one was open for 1% of the time, Pallas kernels for 0%

profile of v2, /device:TPU:4, one launch (start us, length us, event | category | flops | bytes accessed | tf_op | source)
XLA Modules:
  0.0 444.0 jit_solution(9571029984388259739)
XLA Ops:
  7.2 1.7 pad_maximum_fusion
  9.0 147.0 %all-gather.2.cloned.1.call-done.own = bf16[4096,2048]{1,0:T(8,128)(2,1)} async-done(((bf16[64,2048]{1,0:T(8,128)(2,1)}), bf16[4096,2048]{1,0:T(8,128)(2,1)}) %all-gather.2.cloned.1.call-update) | async-done | bytes 16777232 | tf_op jit(solution)/shard_map/all_gather | solution.py:206
  155.9 1.9 collective-permute-start.4
  157.8 2.4 collective-permute-start
  160.3 0.9 dynamic-slice_convert_fusion
  161.2 0.7 pad_maximum_fusion.1.state
  162.5 20.8 %collective-permute-done = f32[2,1024]{1,0:T(2,128)S(1)} collective-permute-done((f32[2,1024]{1,0:T(2,128)}, f32[2,1024]{1,0:T(2,128)S(1)}, u32[]{:S(2)}, u32[]{:S(2)}) %collective-permute-start) | collective-permute-done | bytes 8224 | tf_op jit(solution)/shard_map/ppermute | solution.py:208
  183.3 0.8 maximum_select_fusion.1
  184.1 4.3 collective-permute-start.1
  188.4 5.6 %collective-permute-start.2 = (f32[2,2,1024]{2,1,0:T(2,128)S(1)}, f32[2,2,1024]{2,1,0:T(2,128)S(1)}, u32[]{:S(2)}, u32[]{:S(2)}) collective-permute-start(f32[2,2,1024]{2,1,0:T(2,128)S(1)} %maximum_select_fusion.1), channel_id=1, source_target_pairs={{0,64},{32,96},{64,0},{96,32},{1,65},{33,97},{65,1},{97,33},{2,66}... | collective-permute-start | bytes 49160 | tf_op jit(solution)/shard_map/ppermute | solution.py:211
  194.0 5.4 %collective-permute-start.3 = (f32[2,2,1024]{2,1,0:T(2,128)S(1)}, f32[2,2,1024]{2,1,0:T(2,128)S(1)}, u32[]{:S(2)}, u32[]{:S(2)}) collective-permute-start(f32[2,2,1024]{2,1,0:T(2,128)S(1)} %maximum_select_fusion.1), channel_id=1, source_target_pairs={{0,96},{32,0},{64,32},{96,64},{1,97},{33,1},{65,33},{97,65},{2,98}... | collective-permute-start | bytes 49160 | tf_op jit(solution)/shard_map/ppermute | solution.py:211
  199.4 0.8 maximum_select_fusion
  200.9 0.7 pad_maximum_fusion.2.gains
  201.5 1.1 broadcast_in_dim.18.bnd_in
  202.6 1.6 stage.4
  204.2 1.3 collective-permute-start.5
  206.1 25.4 %collective-permute-done.5.state = bf16[16,4096]{1,0:T(8,128)(2,1)S(1)} collective-permute-done((bf16[16,4096]{1,0:T(8,128)(2,1)}, bf16[16,4096]{1,0:T(8,128)(2,1)S(1)}, u32[]{:S(2)}, u32[]{:S(2)}) %collective-permute-start.5) | collective-permute-done | bytes 131104 | tf_op jit(solution)/shard_map/ppermute | solution.py:227
  231.6 0.7 copy-done.2
  232.2 23.3 %stage.5 = (bf16[8,16,4096]{2,1,0:T(8,128)(2,1)}, bf16[16,4096]{1,0:T(8,128)(2,1)}) custom-call(s32[3]{0:T(128)} %add_add_fusion.2.info, bf16[16,4096]{1,0:T(8,128)(2,1)} %copy-done.2, f32[4,2,2,1024]{3,2,1,0:T(2,128)} %pad_maximum_fusion.2.gains, bf16[4096,2048]{1,0:T(8,128)(2,1)} %all-gather.2.cloned.1.call-done.own, ...), custom_call_target="tpu_custom_call", output_to_operand_aliasing={{0}: (5, {})} | custom-call | flops 1073741824 | bytes 33554432 | tf_op jit(solution)/shard_map/stage/pallas_call | solution.py:134
  255.6 1.3 collective-permute-start.6
  257.5 2.2 collective-permute-done.6.state
  259.7 0.7 copy-done.3
  260.3 1.6 stage.6
  262.0 0.7 collective-permute-start.7
  263.2 0.7 copy-done.1
  263.9 1.8 stage.7
  265.7 34.7 %all_to_all.5 = bf16[8,16,4096]{2,1,0:T(8,128)(2,1)S(1)} all-to-all(bf16[8,16,4096]{2,1,0:T(8,128)(2,1)} %get-tuple-element.22), channel_id=1, replica_groups=mesh['x'=4,'yh'=4,'c'=2,'yl'=2,'z'=8] {'yh','c'}, dimensions={0} | all-to-all | bytes 2097152 | tf_op jit(solution)/shard_map/all_to_all | solution.py:228
  300.4 8.1 %owner.1 = (f32[128,2048]{1,0:T(8,128)}, bf16[128,2048]{1,0:T(8,128)(2,1)}, bf16[1024,2048]{1,0:T(8,128)(2,1)}, f32[2,1024]{1,0:T(2,128)S(1)}) custom-call(s32[1]{0:T(128)} %bitcast.info, bf16[128,4096]{1,0:T(8,128)(2,1)S(1)} %bitcast.23, f32[2,1024]{1,0:T(2,128)S(1)} %bitcast.26, bf16[4096,2048]{1,0:T(8,128)(2,1)} %all-gather.2.cloned.1.call-done.own), custom_call_target="tpu_custom_call" | custom-call | flops 1610612736 | bytes 12582912 | tf_op jit(solution)/shard_map/owner/pallas_call | solution.py:184
  308.5 33.7 %psum.7 = f32[1,2,1024]{2,1,0:T(2,128)} all-reduce(f32[1,2,1024]{2,1,0:T(2,128)S(1)} %bitcast.27), channel_id=1, replica_groups=mesh['x'=4,'yh'=4,'c'=2,'yl'=2,'z'=8] {'yl','z'}, use_global_device_ids=true, to_apply=%region_1.2 | all-reduce | flops 2048 | bytes 16384 | tf_op jit(solution)/shard_map/psum | solution.py:233
  342.2 93.2 %reduce-scatter.2.cloned.1.call-done = bf16[64,2048]{1,0:T(8,128)(2,1)} async-done(((bf16[1024,2048]{1,0:T(8,128)(2,1)}), bf16[64,2048]{1,0:T(8,128)(2,1)}) %reduce-scatter.2.cloned.1.call-update) | async-done | bytes 262160 | tf_op jit(solution)/shard_map/reduce_scatter | solution.py:232
  435.3 1.0 convert_element_type.5
  436.3 0.8 slice_bitcast_fusion
  (18 shorter events, 3.1 us)
Async XLA Ops:
  7.2 148.8 %all-gather.2.cloned.1.call-start = ((), (), s32[]{:S(2)}) async-start(), calls=%async_computation.2 | async-start | bytes 17039360 | tf_op jit(solution)/shard_map/all_gather | solution.py:206
  8.9 426.4 %reduce-scatter.2.cloned.1.call-start = ((), (), s32[]{:S(2)}) async-start(), calls=%async_computation.3 | async-start | bytes 4456448 | tf_op jit(solution)/shard_map/reduce_scatter | solution.py:232
  155.9 45.6 %collective-permute-start.4 = (bf16[4096,2048]{1,0:T(8,128)(2,1)}, bf16[4096,2048]{1,0:T(8,128)(2,1)}, u32[]{:S(2)}, u32[]{:S(2)}) collective-permute-start(bf16[4096,2048]{1,0:T(8,128)(2,1)} %all-gather.2.cloned.1.call-done.own), channel_id=1, source_target_pairs={{0,16},{16,0},{1,17},{17,1},{2,18},{18,2},{3,19},{19,3},{4,20},{20... | collective-permute-start | bytes 50331656 | tf_op jit(solution)/shard_map/ppermute | solution.py:207
  157.8 25.5 %collective-permute-start = (f32[2,1024]{1,0:T(2,128)}, f32[2,1024]{1,0:T(2,128)S(1)}, u32[]{:S(2)}, u32[]{:S(2)}) collective-permute-start(f32[2,1024]{1,0:T(2,128)} %bitcast.24), channel_id=1, source_target_pairs={{0,16},{16,0},{1,17},{17,1},{2,18},{18,2},{3,19},{19,3},{4,20},{20... | collective-permute-start | bytes 24584 | tf_op jit(solution)/shard_map/ppermute | solution.py:208
  184.1 16.1 %collective-permute-start.1 = (f32[2,2,1024]{2,1,0:T(2,128)S(1)}, f32[2,2,1024]{2,1,0:T(2,128)S(1)}, u32[]{:S(2)}, u32[]{:S(2)}) collective-permute-start(f32[2,2,1024]{2,1,0:T(2,128)S(1)} %maximum_select_fusion.1), channel_id=1, source_target_pairs={{0,32},{32,64},{64,96},{96,0},{1,33},{33,65},{65,97},{97,1},{2,34}... | collective-permute-start | bytes 49160 | tf_op jit(solution)/shard_map/ppermute | solution.py:211
  188.4 11.8 %collective-permute-start.2 = (f32[2,2,1024]{2,1,0:T(2,128)S(1)}, f32[2,2,1024]{2,1,0:T(2,128)S(1)}, u32[]{:S(2)}, u32[]{:S(2)}) collective-permute-start(f32[2,2,1024]{2,1,0:T(2,128)S(1)} %maximum_select_fusion.1), channel_id=1, source_target_pairs={{0,64},{32,96},{64,0},{96,32},{1,65},{33,97},{65,1},{97,33},{2,66}... | collective-permute-start | bytes 49160 | tf_op jit(solution)/shard_map/ppermute | solution.py:211
  194.0 6.9 %collective-permute-start.3 = (f32[2,2,1024]{2,1,0:T(2,128)S(1)}, f32[2,2,1024]{2,1,0:T(2,128)S(1)}, u32[]{:S(2)}, u32[]{:S(2)}) collective-permute-start(f32[2,2,1024]{2,1,0:T(2,128)S(1)} %maximum_select_fusion.1), channel_id=1, source_target_pairs={{0,96},{32,0},{64,32},{96,64},{1,97},{33,1},{65,33},{97,65},{2,98}... | collective-permute-start | bytes 49160 | tf_op jit(solution)/shard_map/ppermute | solution.py:211
  204.2 27.3 %collective-permute-start.5 = (bf16[16,4096]{1,0:T(8,128)(2,1)}, bf16[16,4096]{1,0:T(8,128)(2,1)S(1)}, u32[]{:S(2)}, u32[]{:S(2)}) collective-permute-start(bf16[16,4096]{1,0:T(8,128)(2,1)} %get-tuple-element.16), channel_id=1, source_target_pairs={{384,256},{385,257},{386,258},{387,259},{388,260},{389,261},{390,2... | collective-permute-start | bytes 393224 | tf_op jit(solution)/shard_map/ppermute | solution.py:227
  231.6 0.7 copy-start.2
  255.6 4.1 collective-permute-start.6
  259.7 0.7 copy-start.3
  262.0 1.3 collective-permute-start.7
  263.2 0.7 copy-start.1
  263.9 36.5 %copy-start = (f32[1,2,1024]{2,1,0:T(2,128)S(1)}, f32[1,2,1024]{2,1,0:T(2,128)}, u32[]{:S(2)}) copy-start(f32[1,2,1024]{2,1,0:T(2,128)} %param.9) | copy-start | bytes 24580
Sparse Core Ops, SparseCore 0:
  11.6 144.3 all-gather.1
  308.6 126.6 reduce-scatter.1
